TPU v7x, 128 devices: a whole 4x4x4 slice. The times are simulated.
128 devices in a mesh: row: 16 (over y, z), col: 8 (over x, core).
Axes of the slice: x: 4, y: 4, z: 4, core: 2. Of those that a mesh axis runs over, the one named last changes fastest.
Arguments:
- front: bfloat16 [2, 32768, 6144], P(None, 'row', 'col'), may hold values from -6 to 6
- child_tiles: bfloat16 [16384, 2, 128, 128], P(('row', 'col')), may hold values from -6 to 6
- tile_owner: int32 [16384, 1], P(('row', 'col')), may hold values from 0 to 127; in each aligned block of 128 rows (0 to 127, 128 to 255, ...) at most 2 rows name the same one
- tile_spot: int32 [16384], P(('row', 'col')), may hold values from 0 to 95
- tile_count: int32 [128], P(('row', 'col')), may hold values from 96 to 128, as said below
- panel: bfloat16 [2, 32768, 512], P(None, 'row'), may hold values from -0.0234375 to 0.0234375
Outputs:
- assembled: bfloat16 [2, 32768, 6144], P(None, 'row', 'col')
- sample: float32 [2, 512, 6144], P(None, 'row', 'col')
Inputs may be any that keep to these rules, and one draw needn't show every extreme that they name: `tile_owner`: among the 128 tiles of one device, at most 2 name the same owner. `tile_count`: some device holds 128 live tiles.
All inputs are finite; a program needn't handle non-finite values.
Results may differ from a plain program's by a relative error of at most 0.0042.
Values may be sent and summed in bfloat16 or wider, within the bound.
No kernel may reach another device: no remote copies, remote signals or barrier semaphores. Data moves between devices by JAX's collectives and lax.ppermute only.
A program may use at most 256 MiB of HBM per device.

v0:
```python
import functools

import jax
import jax.numpy as jnp
from jax import lax
from jax.experimental import pallas as pl
from jax.experimental.pallas import tpu as pltpu
from jax.sharding import PartitionSpec as P

BOTH = ("row", "col")
VMEM_LIMIT = 60 * 1024 * 1024


def pack(n_dev, owner, spot, count, tiles, out, held, labels, sem_in, sem_out, sem_labels, seen, slot_of, spots):
    live = jnp.minimum(count[0], tiles.shape[0])

    def clear(d, carry):
        seen[d] = 0
        for k in range(2):
            spots[d * 2 + k] = -1
        return carry

    lax.fori_loop(0, n_dev, clear, 0, unroll=8)

    def fetch(j):
        return pltpu.make_async_copy(tiles.at[j], held.at[j], sem_in.at[j])

    def forward(j):
        slot = slot_of[j]
        to = slot // 2
        here = out.at[to, pl.ds(pl.multiple_of((slot - to * 2) * 256, 256), 256)]
        return pltpu.make_async_copy(held.at[j], here, sem_out.at[j])

    def route(j, carry):
        fetch(j).start()
        to = owner[j]
        rank = seen[to]
        seen[to] = rank + 1
        slot_of[j] = to * 2 + rank
        spots[to * 2 + rank] = spot[j]
        return carry

    lax.fori_loop(0, live, route, 0)

    def pass_on(j, carry):
        fetch(j).wait()
        forward(j).start()
        return carry

    lax.fori_loop(0, live, pass_on, 0)
    lane = lax.broadcasted_iota(jnp.int32, (8, 128), 1)

    def label(d, carry):
        row = jnp.where(lane == 0, spots[d * 2], jnp.where(lane == 1, spots[d * 2 + 1], 0))
        labels[d] = row.astype(jnp.float32).astype(jnp.bfloat16)
        return carry

    lax.fori_loop(0, n_dev, label, 0, unroll=4)
    send_labels = pltpu.make_async_copy(labels, out.at[:, pl.ds(512, 8)], sem_labels)
    send_labels.start()

    def finish(j, carry):
        forward(j).wait()
        return carry

    lax.fori_loop(0, live, finish, 0)
    send_labels.wait()


def extend_add(cols_blocks, ahead, order, starts, front, tiles, assembled, held, sem):
    step = pl.program_id(0)
    steps = pl.num_programs(0)

    def fetch(p):
        slot = order[p]
        source = slot // 2
        here = tiles.at[source, pl.ds(pl.multiple_of((slot - source * 2) * 256, 256), 256)]
        return pltpu.make_async_copy(here, held.at[p], sem.at[p])

    def begin(p, carry):
        fetch(p).start()
        return carry

    def arrive(p, carry):
        fetch(p).wait()
        return carry

    def fence(s):
        return starts[s * cols_blocks]

    @pl.when(step == 0)
    def _():
        lax.fori_loop(0, fence(ahead), begin, 0)

    @pl.when(step + ahead < steps)
    def _():
        lax.fori_loop(fence(step + ahead), fence(step + ahead + 1), begin, 0)

    lax.fori_loop(fence(step), fence(step + 1), arrive, 0)
    for c in range(cols_blocks):
        first, last = starts[step * cols_blocks + c], starts[step * cols_blocks + c + 1]
        for part in range(2):

            def add(p, value):
                return value + held[p, part * 128 : (part + 1) * 128, :].astype(jnp.float32)

            here = (part, slice(None), slice(c * 128, (c + 1) * 128))
            value = lax.fori_loop(first, last, add, front[here].astype(jnp.float32))
            assembled[here] = value.astype(jnp.bfloat16)


def body(front, child_tiles, tile_owner, tile_spot, tile_count, panel):
    n_row = lax.axis_size("row")
    n_dev = n_row * lax.axis_size("col")
    n_tiles = child_tiles.shape[0]
    tile = child_tiles.shape[2]
    height, width = front.shape[1:]
    rows_blocks, cols_blocks = height // tile, width // tile
    n_spots = rows_blocks * cols_blocks
    samples = panel.shape[2]
    f32, bf16, i32 = jnp.float32, jnp.bfloat16, jnp.int32
    smem = pl.BlockSpec(memory_space=pltpu.SMEM)
    hbm = pl.BlockSpec(memory_space=pl.ANY)
    params = functools.partial(pltpu.CompilerParams, vmem_limit_bytes=VMEM_LIMIT)
    n_slots = 2 * n_dev
    message = 4 * tile + 8

    packed = pl.pallas_call(
        functools.partial(pack, n_dev),
        out_shape=jax.ShapeDtypeStruct((n_dev, message, tile), bf16),
        in_specs=[smem, smem, smem, hbm],
        out_specs=hbm,
        scratch_shapes=[
            pltpu.VMEM((n_tiles, 2 * tile, tile), bf16),
            pltpu.VMEM((n_dev, 8, tile), bf16),
            pltpu.SemaphoreType.DMA((n_tiles,)),
            pltpu.SemaphoreType.DMA((n_tiles,)),
            pltpu.SemaphoreType.DMA,
            pltpu.SMEM((n_dev,), i32),
            pltpu.SMEM((n_tiles,), i32),
            pltpu.SMEM((n_slots,), i32),
        ],
        compiler_params=params(),
        cost_estimate=pl.CostEstimate(flops=1 << 20, bytes_accessed=2 * n_dev * 65536, transcendentals=0),
        name="pack",
    )(tile_owner[:, 0], tile_spot, tile_count, child_tiles.reshape(n_tiles, 2 * tile, tile))
    got = lax.all_to_all(packed, BOTH, split_axis=0, concat_axis=0, tiled=True)

    spots = got[:, 4 * tile, :2].astype(i32).reshape(n_slots)
    slot = jnp.arange(n_slots, dtype=i32)
    key = jnp.where(spots >= 0, spots, n_spots) * n_slots + slot
    place = jnp.sum((key[None, :] < key[:, None]).astype(i32), axis=1)
    order = jnp.sum(jnp.where(place[None, :] == slot[:, None], slot[None, :], 0), axis=1)
    starts = jnp.sum((key[None, :] < (jnp.arange(n_spots + 1) * n_slots)[:, None]).astype(i32), axis=1)

    turned = panel.transpose(2, 0, 1)
    crossed = jnp.stack([-turned[:, 1], turned[:, 0]], axis=1)
    weights = jnp.stack([turned.reshape(n_row, -1, 2 * height), crossed.reshape(n_row, -1, 2 * height)], axis=1)
    weights = weights.reshape(2 * samples, 2 * height)

    ahead = 2
    assembled = pl.pallas_call(
        functools.partial(extend_add, cols_blocks, ahead),
        grid=(rows_blocks,),
        out_shape=jax.ShapeDtypeStruct((2, height, width), bf16),
        in_specs=[
            smem,
            smem,
            pl.BlockSpec((2, tile, width), lambda i: (0, i, 0)),
            hbm,
        ],
        out_specs=pl.BlockSpec((2, tile, width), lambda i: (0, i, 0)),
        scratch_shapes=[
            pltpu.VMEM((n_slots, 2 * tile, tile), bf16),
            pltpu.SemaphoreType.DMA((n_slots,)),
        ],
        compiler_params=params(),
        cost_estimate=pl.CostEstimate(flops=8 << 30, bytes_accessed=28 << 20, transcendentals=0),
        name="extend_add",
    )(order, starts, front, got)

    partial = jnp.dot(weights, assembled.reshape(2 * height, width), preferred_element_type=f32).astype(bf16)
    arrived = lax.all_to_all(
        partial.reshape(n_row, 2 * samples // n_row, width), "row", split_axis=0, concat_axis=0, tiled=True
    )
    sample = arrived.astype(f32).sum(axis=0).reshape(2, samples // n_row, width)
    return assembled, sample


def solution(mesh):
    placed = (
        P(None, "row", "col"),
        P(BOTH, None, None, None),
        P(BOTH, None),
        P(BOTH),
        P(BOTH),
        P(None, "row", None),
    )
    return jax.shard_map(
        body,
        mesh=mesh,
        in_specs=placed,
        out_specs=(P(None, "row", "col"), P(None, "row", "col")),
        check_vma=False,
    )
```

profile of v0, /device:TPU:2, one launch (start us, length us, event | category | flops | bytes accessed | tf_op | source)
XLA Modules:
  0.0 324.2 jit_solution(2171881068126849874)
XLA Ops:
  1.3 9.1 %pack.1 = bf16[128,520,128]{2,1,0:T(8,128)(2,1)} custom-call(s32[128]{0:T(128)} %bitcast.15, s32[128]{0:T(128)} %spot.1, s32[1]{0:T(128)S(6)} %copy.14.count, bf16[128,256,128]{2,1,0:T(8,128)(2,1)} %bitcast.12), custom_call_target="tpu_custom_call" | custom-call | flops 1048576 | bytes 16777216 | tf_op jit(solution)/shard_map/pack/pallas_call | solution.py:128
  10.4 11.6 %all-to-all-start = ((bf16[128,520,128]{2,1,0:T(8,128)(2,1)}), bf16[128,520,128]{2,1,0:T(8,128)(2,1)}, u32[]{:S(2)}, u32[]{:S(2)}) async-start(bf16[128,520,128]{2,1,0:T(8,128)(2,1)} %pack.1), calls=%async_computation | async-start | bytes 34078720 | tf_op jit(solution)/shard_map/all_to_all | solution.py:147
  22.0 11.4 %copy.11 = bf16[512,2,2048]{2,1,0:T(2,128)(2,1)} copy(bf16[512,2,2048]{0,2,1:T(8,128)(2,1)} %bitcast.9) | data formatting | bytes 8388608 | tf_op jit(solution)/shard_map/transpose | solution.py:156
  33.4 2.5 slice_negate_fusion
  35.9 2.4 pad_maximum_fusion.1
  38.3 11.4 %copy.12 = bf16[512,2,2048]{2,1,0:T(2,128)(2,1)} copy(bf16[512,2,2048]{0,2,1:T(8,128)(2,1)} %pad_maximum_fusion.1) | data formatting | bytes 8388608 | tf_op jit(solution)/shard_map/stack | solution.py:157
  49.7 7.8 %stack_reshape.7 = bf16[16,1,32,4096]{3,2,0,1:T(8,128)(2,1)} reshape(bf16[512,2,2048]{2,1,0:T(2,128)(2,1)} %copy.12) | data formatting | bytes 8388608 | tf_op jit(solution)/shard_map/stack;reshape | solution.py:158
  57.4 7.8 %stack_reshape.6 = bf16[16,1,32,4096]{3,2,0,1:T(8,128)(2,1)} reshape(bf16[512,2,2048]{2,1,0:T(2,128)(2,1)} %copy.11) | data formatting | bytes 8388608 | tf_op jit(solution)/shard_map/stack;reshape | solution.py:158
  65.2 7.4 %pad_maximum_fusion = bf16[16,2,32,4096]{3,2,0,1:T(8,128)(2,1)} fusion(bf16[16,1,32,4096]{3,2,0,1:T(8,128)(2,1)} %stack_reshape.7, bf16[16,1,32,4096]{3,2,0,1:T(8,128)(2,1)} %stack_reshape.6), kind=kLoop, calls=%fused_computation | loop fusion | flops 4194304 | bytes 16777216 | tf_op jit(solution)/shard_map/stack | solution.py:158
  72.7 7.7 %copy.13 = bf16[16,2,32,4096]{3,2,1,0:T(8,128)(2,1)} copy(bf16[16,2,32,4096]{3,2,0,1:T(8,128)(2,1)} %pad_maximum_fusion) | data formatting | bytes 16777216 | tf_op jit(solution)/shard_map/stack | solution.py:158
  80.4 175.5 %all-to-all-done.tiles = bf16[128,520,128]{2,1,0:T(8,128)(2,1)} async-done(((bf16[128,520,128]{2,1,0:T(8,128)(2,1)}), bf16[128,520,128]{2,1,0:T(8,128)(2,1)}, u32[]{:S(2)}, u32[]{:S(2)}) %all-to-all-start) | async-done | bytes 17039392 | tf_op jit(solution)/shard_map/all_to_all | solution.py:147
  256.0 1.2 fusion
  257.1 0.1 reshape.57
  257.3 0.2 convert_reduce_fusion.1
  257.5 0.7 select_reduce_fusion.order
  258.1 0.7 convert_reduce_fusion.2.starts
  258.9 16.8 %extend_add.1 = bf16[2,2048,768]{2,1,0:T(8,128)(2,1)} custom-call(s32[256]{0:T(256)} %select_reduce_fusion.order, s32[97]{0:T(128)} %convert_reduce_fusion.2.starts, bf16[2,2048,768]{2,1,0:T(8,128)(2,1)} %front.1, bf16[128,520,128]{2,1,0:T(8,128)(2,1)} %all-to-all-done.tiles), custom_call_target="tpu_custom_call" | custom-call | flops 8589934592 | bytes 29360128 | tf_op jit(solution)/shard_map/extend_add/pallas_call | solution.py:162
  275.7 10.9 %convolution_convert_fusion = bf16[1024,768]{1,0:T(8,128)(2,1)S(1)} fusion(bf16[1024,4096]{1,0:T(8,128)(2,1)} %bitcast.11, bf16[4096,768]{1,0:T(8,128)(2,1)} %bitcast.16), kind=kOutput, calls=%fused_computation.4 | convolution fusion | flops 6443237376 | bytes 16252928 | tf_op jit(solution)/shard_map/dot_general | solution.py:182
  286.6 36.7 %all_to_all.10 = bf16[16,64,768]{2,1,0:T(8,128)(2,1)S(1)} all-to-all(bf16[16,64,768]{2,1,0:T(8,128)(2,1)S(1)} %bitcast.13), channel_id=1, replica_groups=mesh['row'=16,'col'=8] {'row'}, dimensions={0} | all-to-all | bytes 3145728 | tf_op jit(solution)/shard_map/all_to_all | solution.py:183
  323.3 0.9 convert_reduce_fusion
  (2 shorter events, 0.0 us)
Async XLA Ops:
  10.4 245.6 %all-to-all-start = ((bf16[128,520,128]{2,1,0:T(8,128)(2,1)}), bf16[128,520,128]{2,1,0:T(8,128)(2,1)}, u32[]{:S(2)}, u32[]{:S(2)}) async-start(bf16[128,520,128]{2,1,0:T(8,128)(2,1)} %pack.1), calls=%async_computation | async-start | bytes 34078720 | tf_op jit(solution)/shard_map/all_to_all | solution.py:147
where the time goes:
time: 329 us; the launch traced here: 324 us
  waiting for transfers between devices  176 us (53%)
  local copies, waits for them, and re-layouts  46.2 us (14%)
  blocking collectives  36.7 us (11%)
  Pallas kernels  25.9 us (8%)
  other arithmetic  16 us (5%)
  starting transfers between devices  11.6 us (4%)
  matrix products  10.9 us (3%)
    all_to_all x1, waiting for transfers between devices, body(): got = lax.all_to_all(packed, BOTH, split_axis=0, concat_axis=0, tiled=True)  176 us
    all_to_all x1, blocking collectives, body(): lax.all_to_all(partial.reshape(n_row, 2 * samples // n_row, width), 'row'...  36.7 us
    another operation x3, local copies, waits for them, and re-layouts, body(): jnp.stack([turned.reshape(n_row, -1, 2 * height), crossed.reshape(n_row,...  23.3 us
    pallas_call x1, Pallas kernels, body(): pl.pallas_call(functools.partial(extend_add, cols_blocks, ahead), grid=(r...  16.8 us
    all_to_all x1, starting transfers between devices, body(): got = lax.all_to_all(packed, BOTH, split_axis=0, concat_axis=0, tiled=True)  11.6 us
    transpose x1, local copies, waits for them, and re-layouts, body(): turned = panel.transpose(2, 0, 1)  11.4 us
    another operation x1, local copies, waits for them, and re-layouts, body(): crossed = jnp.stack([-turned[:, 1], turned[:, 0]], axis=1)  11.4 us
    dot_general x1, matrix products, body(): jnp.dot(weights, assembled.reshape(2 * height, width), preferred_element_...  10.9 us
  transfers between devices with their start and end apart: 1, of which 1 were waited for; matrix products, arithmetic and copies ran while one was open for 18% of the time, Pallas kernels for 0%

commit v1 on v0

v1 whole, which is shorter than its diff:
```python
import functools

import jax
import jax.numpy as jnp
from jax import lax
from jax.experimental import pallas as pl
from jax.experimental.pallas import tpu as pltpu
from jax.sharding import PartitionSpec as P

BOTH = ("row", "col")
VMEM_LIMIT = 4 * 1024 * 1024


def pack(n_dev, owner, spot, count, tiles, out, sem, seen, slot_of, spots):
    live = jnp.minimum(count[0], tiles.shape[0])

    def clear(d, carry):
        seen[d] = 0
        for k in range(2):
            spots[d * 2 + k] = -1
        return carry

    lax.fori_loop(0, n_dev, clear, 0, unroll=8)

    def fetch(j, to, rank):
        here = out.at[to, pl.ds(pl.multiple_of(rank * 256, 256), 256)]
        return pltpu.make_async_copy(tiles.at[j], here, sem.at[j])

    def route(j, carry):
        to = owner[j]
        rank = seen[to]
        fetch(j, to, rank).start()
        seen[to] = rank + 1
        slot_of[j] = to * 2 + rank
        spots[to * 2 + rank] = spot[j]
        return carry

    lax.fori_loop(0, live, route, 0)
    lane = lax.broadcasted_iota(jnp.int32, (8, 128), 1)

    def label(d, carry):
        row = jnp.where(lane == 0, spots[d * 2], jnp.where(lane == 1, spots[d * 2 + 1], 0))
        out[d, 512:520, :] = row.astype(jnp.float32).astype(jnp.bfloat16)
        return carry

    lax.fori_loop(0, n_dev, label, 0, unroll=4)

    def finish(j, carry):
        slot = slot_of[j]
        to = slot // 2
        fetch(j, to, slot - to * 2).wait()
        return carry

    lax.fori_loop(0, live, finish, 0)


def extend_add(n_dev, rows_blocks, cols_blocks, order, starts, tiles, front, assembled, rounded, sem):
    def rows(step):
        return pl.ds(pl.multiple_of(step * 128, 128), 128)

    def put(step):
        turn = step % 2
        return pltpu.make_async_copy(rounded.at[turn], assembled.at[:, rows(step)], sem.at[turn])

    def one(step, carry):
        turn = step % 2

        @pl.when(step >= 2)
        def _():
            put(step - 2).wait()

        for c in range(cols_blocks):
            first, last = starts[step * cols_blocks + c], starts[step * cols_blocks + c + 1]
            columns = slice(c * 128, (c + 1) * 128)
            for part in range(2):

                def add(p, value):
                    slot = order[p]
                    rank = slot // n_dev
                    here = pl.ds(pl.multiple_of(rank * 256 + part * 128, 128), 128)
                    return value + tiles[slot - rank * n_dev, here, :].astype(jnp.float32)

                value = lax.fori_loop(first, last, add, front[part, rows(step), columns].astype(jnp.float32))
                rounded[turn, part, :, columns] = value.astype(jnp.bfloat16)
        put(step).start()
        return carry

    lax.fori_loop(0, rows_blocks, one, 0)
    for step in (rows_blocks - 2, rows_blocks - 1):
        put(step).wait()


def body(front, child_tiles, tile_owner, tile_spot, tile_count, panel):
    n_row = lax.axis_size("row")
    n_dev = n_row * lax.axis_size("col")
    n_tiles = child_tiles.shape[0]
    tile = child_tiles.shape[2]
    height, width = front.shape[1:]
    rows_blocks, cols_blocks = height // tile, width // tile
    n_spots = rows_blocks * cols_blocks
    samples = panel.shape[2]
    f32, bf16, i32 = jnp.float32, jnp.bfloat16, jnp.int32
    smem = pl.BlockSpec(memory_space=pltpu.SMEM)
    hbm = pl.BlockSpec(memory_space=pltpu.HBM)
    vmem = pl.BlockSpec(memory_space=pltpu.VMEM)
    params = functools.partial(pltpu.CompilerParams, vmem_limit_bytes=VMEM_LIMIT)
    n_slots = 2 * n_dev
    message = 4 * tile + 8

    packed = pl.pallas_call(
        functools.partial(pack, n_dev),
        out_shape=jax.ShapeDtypeStruct((n_dev, message, tile), bf16),
        in_specs=[smem, smem, smem, hbm],
        out_specs=vmem,
        scratch_shapes=[
            pltpu.SemaphoreType.DMA((n_tiles,)),
            pltpu.SMEM((n_dev,), i32),
            pltpu.SMEM((n_tiles,), i32),
            pltpu.SMEM((n_slots,), i32),
        ],
        compiler_params=params(),
        cost_estimate=pl.CostEstimate(flops=1 << 20, bytes_accessed=2 * n_dev * 65536, transcendentals=0),
        name="pack",
    )(tile_owner[:, 0], tile_spot, tile_count, child_tiles.reshape(n_tiles, 2 * tile, tile))
    got = lax.all_to_all(packed, BOTH, split_axis=0, concat_axis=0, tiled=True)

    spots = jnp.concatenate([got[:, 4 * tile, 0], got[:, 4 * tile, 1]]).astype(i32)
    slot = jnp.arange(n_slots, dtype=i32)
    spots = jnp.where(spots >= 0, spots, n_spots)
    key = spots * n_slots + slot
    place = jnp.sum((key[None, :] < key[:, None]).astype(i32), axis=1)
    order = jnp.sum(jnp.where(place[None, :] == slot[:, None], slot[None, :], 0), axis=1)
    starts = jnp.sum((spots[None, :] < jnp.arange(n_spots + 1)[:, None]).astype(i32), axis=1)

    assembled = pl.pallas_call(
        functools.partial(extend_add, n_dev, rows_blocks, cols_blocks),
        out_shape=jax.ShapeDtypeStruct((2, height, width), bf16),
        in_specs=[smem, smem, vmem, vmem],
        out_specs=hbm,
        scratch_shapes=[
            pltpu.VMEM((2, 2, tile, width), bf16),
            pltpu.SemaphoreType.DMA((2,)),
        ],
        compiler_params=params(),
        cost_estimate=pl.CostEstimate(flops=8 << 30, bytes_accessed=28 << 20, transcendentals=0),
        name="extend_add",
    )(order, starts, got, front)

    def product(p, a):
        return lax.dot_general(p, a, (((0,), (0,)), ((), ())), preferred_element_type=f32)

    real = product(panel.reshape(2 * height, samples), assembled.reshape(2 * height, width))
    imag = product(panel[0], assembled[1]) - product(panel[1], assembled[0])
    partial = jnp.stack([real.astype(bf16).reshape(n_row, -1, width), imag.astype(bf16).reshape(n_row, -1, width)], axis=1)
    arrived = lax.all_to_all(
        partial.reshape(n_row, 2 * samples // n_row, width), "row", split_axis=0, concat_axis=0, tiled=True
    )
    sample = arrived.astype(f32).sum(axis=0).reshape(2, samples // n_row, width)
    return assembled, sample


def solution(mesh):
    placed = (
        P(None, "row", "col"),
        P(BOTH, None, None, None),
        P(BOTH, None),
        P(BOTH),
        P(BOTH),
        P(None, "row", None),
    )
    return jax.shard_map(
        body,
        mesh=mesh,
        in_specs=placed,
        out_specs=(P(None, "row", "col"), P(None, "row", "col")),
        check_vma=False,
    )
```

time: 329 us -> 277 us (0.84); the launches traced: 324 us -> 277 us
  blocking collectives: 36.7 us -> 234 us
  waiting for transfers between devices: 176 us -> 0 us
  local copies, waits for them, and re-layouts: 46.2 us -> 6.29 us
  other arithmetic: 16 us -> 1.48 us
  starting transfers between devices: 11.6 us -> 0 us
    all_to_all x0 -> x1, blocking collectives: none -> 205 us  [body(): got = lax.all_to_all(packed, BOTH, split_axis=0, concat_axis=0, tiled=True)]
    all_to_all x1 -> x0, waiting for transfers between devices: 176 us -> none  [body(): got = lax.all_to_all(packed, BOTH, split_axis=0, concat_axis=0, tiled=True)]
    another operation x4 -> x0, local copies, waits for them, and re-layouts: 34.7 us -> none  [the longest x3 23.3 us: body(): jnp.stack([turned.reshape(n_row, -1, 2 * height), crossed.reshape(n_row,...]
    all_to_all x1 -> x0, starting transfers between devices: 11.6 us -> none  [body(): got = lax.all_to_all(packed, BOTH, split_axis=0, concat_axis=0, tiled=True)]
    transpose x1 -> x0, local copies, waits for them, and re-layouts: 11.4 us -> none  [body(): turned = panel.transpose(2, 0, 1)]
    another operation x2 -> x1, other arithmetic: 9.82 us -> 0.15 us  [body(): jnp.stack([real.astype(bf16).reshape(n_row, -1, width), imag.astype(bf16)...]
    all_to_all x1, blocking collectives: 36.7 us -> 29.6 us  [body(): lax.all_to_all(partial.reshape(n_row, 2 * samples // n_row, width), 'row'...]
    pallas_call x1, Pallas kernels: 16.8 us -> 9.68 us  [body(): pl.pallas_call(functools.partial(extend_add, n_dev, rows_blocks, cols_blo...]
  transfers between devices with their start and end apart: 1 -> 0, of which waited for: 1 -> 0; matrix products, arithmetic and copies ran while one was open for 18% -> 0% of each run, Pallas kernels for 0% -> 0%
where the time goes in v1:
time: 277 us
  blocking collectives  234 us (84%)
  Pallas kernels  23.5 us (8%)
  matrix products  9.83 us (4%)
  local copies, waits for them, and re-layouts  6.29 us (2%)
    all_to_all x1, blocking collectives, body(): got = lax.all_to_all(packed, BOTH, split_axis=0, concat_axis=0, tiled=True)  205 us
    all_to_all x1, blocking collectives, body(): lax.all_to_all(partial.reshape(n_row, 2 * samples // n_row, width), 'row'...  29.6 us
    pallas_call x1, Pallas kernels, body(): pl.pallas_call(functools.partial(pack, n_dev), out_shape=jax.ShapeDtypeSt...  13.8 us
    dot_general x3, matrix products, product(): lax.dot_general(p, a, (((0,), (0,)), ((), ())), preferred_element_type=f32)  9.83 us
    pallas_call x1, Pallas kernels, body(): pl.pallas_call(functools.partial(extend_add, n_dev, rows_blocks, cols_blo...  9.68 us

profile of v1, /device:TPU:2, one launch (start us, length us, event | category | flops | bytes accessed | tf_op | source)
XLA Modules:
  0.0 276.6 jit_solution(16150505187004518928)
XLA Ops:
  1.3 0.0 copy-start
  1.3 3.4 %copy-done = bf16[128,2,128,128]{3,2,1,0:T(8,128)(2,1)S(1)} copy-done((bf16[128,2,128,128]{3,2,1,0:T(8,128)(2,1)S(1)}, bf16[128,2,128,128]{3,2,1,0:T(8,128)(2,1)}, u32[]{:S(2)}) %copy-start) | copy-done | bytes 8388632
  4.7 0.7 copy-done.1
  5.3 0.7 copy-done.2
  6.0 13.8 %pack.1 = bf16[128,520,128]{2,1,0:T(8,128)(2,1)S(1)} custom-call(s32[128]{0:T(128)S(1)} %bitcast.35, s32[128]{0:T(128)S(1)} %copy-done.2, s32[1]{0:T(128)S(6)} %copy.16.count, bf16[128,256,128]{2,1,0:T(8,128)(2,1)S(1)} %bitcast.34), custom_call_target="tpu_custom_call" | custom-call | flops 1048576 | bytes 16777216 | tf_op jit(solution)/shard_map/pack/pallas_call | solution.py:110
  19.8 0.0 slice-start.1
  19.8 204.6 %all_to_all.10.tiles = bf16[128,520,128]{2,1,0:T(8,128)(2,1)S(1)} all-to-all(bf16[128,520,128]{2,1,0:T(8,128)(2,1)S(1)} %pack.1), channel_id=1, replica_groups=mesh['row'=16,'col'=8] {'row','col'}, dimensions={0} | all-to-all | bytes 34078720 | tf_op jit(solution)/shard_map/all_to_all | solution.py:125
  224.3 1.6 slice_reduce_fusion.1
  225.9 0.1 convert_reduce_fusion.2.starts
  226.0 0.2 convert_reduce_fusion.1
  226.2 0.1 select_reduce_fusion.order
  226.4 0.0 slice-done
  226.4 0.0 slice-done.1
  226.4 0.0 copy-start.3
  226.4 9.7 %extend_add.1 = bf16[2,2048,768]{2,1,0:T(8,128)(2,1)} custom-call(s32[256]{0:T(256)S(1)} %select_reduce_fusion.order, s32[97]{0:T(128)S(1)} %convert_reduce_fusion.2.starts, bf16[128,520,128]{2,1,0:T(8,128)(2,1)S(1)} %all_to_all.10.tiles, bf16[2,2048,768]{2,1,0:T(8,128)(2,1)S(1)} %bitcast.37), custom_call_target="tpu_custom_call" | custom-call | flops 8589934592 | bytes 29360128 | tf_op jit(solution)/shard_map/extend_add/pallas_call | solution.py:135
  236.1 0.0 copy-done.3
  236.1 0.0 copy-start.4
  236.1 5.9 %bitcast_convert_fusion = bf16[768,512]{0,1:T(8,128)(2,1)S(1)} fusion(bf16[2,2048,768]{2,1,0:T(8,128)(2,1)} %extend_add.1, bf16[2,2048,512]{2,1,0:T(8,128)(2,1)S(1)} %copy-done.3), kind=kOutput, calls=%fused_computation.10 | convolution fusion | flops 3221618688 | bytes 11272192 | tf_op jit(solution)/shard_map/dot_general | solution.py:150
  242.1 0.0 copy-done.4
  242.1 1.9 fusion
  244.0 1.9 subtract_convert_fusion
  246.0 0.2 pad_maximum_fusion
  246.1 29.6 %all_to_all.11 = bf16[16,64,768]{2,1,0:T(8,128)(2,1)S(1)} all-to-all(bf16[16,64,768]{2,1,0:T(8,128)(2,1)S(1)} %bitcast.38), channel_id=1, replica_groups=mesh['row'=16,'col'=8] {'row'}, dimensions={0} | all-to-all | bytes 3145728 | tf_op jit(solution)/shard_map/all_to_all | solution.py:155
  275.7 0.9 convert_reduce_fusion
  (5 shorter events, 0.0 us)
Async XLA Ops:
  1.3 3.4 %copy-start = (bf16[128,2,128,128]{3,2,1,0:T(8,128)(2,1)S(1)}, bf16[128,2,128,128]{3,2,1,0:T(8,128)(2,1)}, u32[]{:S(2)}) copy-start(bf16[128,2,128,128]{3,2,1,0:T(8,128)(2,1)} %param.7) | copy-start | bytes 25165828
  4.7 0.7 copy-start.1
  5.3 0.7 copy-start.2
  6.0 220.4 %slice-start = ((s8[6291456]{0:T(1024)(128)(4,1)}), s8[4194304]{0:T(1024)(128)(4,1)S(1)}, s32[]{:S(2)}) async-start(s8[6291456]{0:T(1024)(128)(4,1)} %bitcast.36), calls=%async_computation.2 | async-start | bytes 8388608
  19.8 206.6 %slice-start.1 = ((s8[6291456]{0:T(1024)(128)(4,1)}), s8[2097152]{0:T(1024)(128)(4,1)S(1)}, s32[]{:S(2)}) async-start(s8[6291456]{0:T(1024)(128)(4,1)} %bitcast.36), calls=%async_computation.3 | async-start | bytes 4194304
  226.4 9.7 %copy-start.3 = (bf16[2,2048,512]{2,1,0:T(8,128)(2,1)S(1)}, bf16[2,2048,512]{2,1,0:T(8,128)(2,1)}, u32[]{:S(2)}) copy-start(bf16[2,2048,512]{2,1,0:T(8,128)(2,1)} %param.11) | copy-start | bytes 12582916
  236.1 6.0 %copy-start.4 = (bf16[2,2048,768]{2,1,0:T(8,128)(2,1)S(1)}, bf16[2,2048,768]{2,1,0:T(8,128)(2,1)}, u32[]{:S(2)}) copy-start(bf16[2,2048,768]{2,1,0:T(8,128)(2,1)} %extend_add.1) | copy-start | bytes 18874372

commit v2 on v1

v2 whole, which is shorter than its diff:
```python
import functools

import jax
import jax.numpy as jnp
from jax import lax
from jax.experimental import pallas as pl
from jax.experimental.pallas import tpu as pltpu
from jax.sharding import PartitionSpec as P

BOTH = ("row", "col")
VMEM_LIMIT = 4 * 1024 * 1024


def pack(n_dev, owner, spot, count, tiles, out, seen, spots):
    def clear(d, carry):
        seen[d] = 0
        for k in range(2):
            spots[d * 2 + k] = -1
        return carry

    lax.fori_loop(0, n_dev, clear, 0, unroll=8)

    def route(j, carry):
        to = owner[j]
        rank = seen[to]
        seen[to] = rank + 1
        spots[to * 2 + rank] = spot[j]
        out[to, pl.ds(pl.multiple_of(rank * 256, 256), 256), :] = tiles[j]
        return carry

    lax.fori_loop(0, jnp.minimum(count[0], tiles.shape[0]), route, 0)
    lane = lax.broadcasted_iota(jnp.int32, (8, 128), 1)

    def label(d, carry):
        row = jnp.where(lane == 0, spots[d * 2], jnp.where(lane == 1, spots[d * 2 + 1], 0))
        out[d, 512:520, :] = row.astype(jnp.float32).astype(jnp.bfloat16)
        return carry

    lax.fori_loop(0, n_dev, label, 0, unroll=4)


def extend_add(n_dev, rows_blocks, cols_blocks, order, starts, tiles, front, assembled, near, sem):
    def rows(step):
        return pl.ds(pl.multiple_of(step * 128, 128), 128)

    def put(step):
        return pltpu.make_async_copy(near.at[:, rows(step)], assembled.at[:, rows(step)], sem.at[step])

    def one(step, carry):
        for c in range(cols_blocks):
            first, last = starts[step * cols_blocks + c], starts[step * cols_blocks + c + 1]
            columns = slice(c * 128, (c + 1) * 128)

            def add(p, values):
                slot = order[p]
                rank = slot // n_dev
                source = slot - rank * n_dev
                return tuple(
                    value + tiles[source, pl.ds(pl.multiple_of(rank * 256 + part * 128, 128), 128), :].astype(jnp.float32)
                    for part, value in enumerate(values)
                )

            values = tuple(front[part, rows(step), columns].astype(jnp.float32) for part in range(2))
            for part, value in enumerate(lax.fori_loop(first, last, add, values)):
                near[part, rows(step), columns] = value.astype(jnp.bfloat16)
        put(step).start()
        return carry

    def finish(step, carry):
        put(step).wait()
        return carry

    lax.fori_loop(0, rows_blocks, one, 0)
    lax.fori_loop(0, rows_blocks, finish, 0)


def body(front, child_tiles, tile_owner, tile_spot, tile_count, panel):
    n_row = lax.axis_size("row")
    n_dev = n_row * lax.axis_size("col")
    n_tiles = child_tiles.shape[0]
    tile = child_tiles.shape[2]
    height, width = front.shape[1:]
    rows_blocks, cols_blocks = height // tile, width // tile
    n_spots = rows_blocks * cols_blocks
    samples = panel.shape[2]
    f32, bf16, i32 = jnp.float32, jnp.bfloat16, jnp.int32
    smem = pl.BlockSpec(memory_space=pltpu.SMEM)
    vmem = pl.BlockSpec(memory_space=pltpu.VMEM)
    params = functools.partial(pltpu.CompilerParams, vmem_limit_bytes=VMEM_LIMIT)
    n_slots = 2 * n_dev
    message = 4 * tile + 8

    packed = pl.pallas_call(
        functools.partial(pack, n_dev),
        out_shape=jax.ShapeDtypeStruct((n_dev, message, tile), bf16),
        in_specs=[smem, smem, smem, vmem],
        out_specs=vmem,
        scratch_shapes=[pltpu.SMEM((n_dev,), i32), pltpu.SMEM((n_slots,), i32)],
        compiler_params=params(),
        cost_estimate=pl.CostEstimate(flops=1 << 20, bytes_accessed=2 * n_dev * 65536, transcendentals=0),
        name="pack",
    )(tile_owner[:, 0], tile_spot, tile_count, child_tiles.reshape(n_tiles, 2 * tile, tile))
    got = lax.all_to_all(packed, BOTH, split_axis=0, concat_axis=0, tiled=True)

    spots = jnp.concatenate([got[:, 4 * tile, 0], got[:, 4 * tile, 1]]).astype(i32)
    slot = jnp.arange(n_slots, dtype=i32)
    spots = jnp.where(spots >= 0, spots, n_spots)
    key = spots * n_slots + slot
    place = jnp.sum((key[None, :] < key[:, None]).astype(i32), axis=1)
    order = jnp.sum(jnp.where(place[None, :] == slot[:, None], slot[None, :], 0), axis=1)
    starts = jnp.sum((spots[None, :] < jnp.arange(n_spots + 1)[:, None]).astype(i32), axis=1)

    result = jax.ShapeDtypeStruct((2, height, width), bf16)
    assembled, near = pl.pallas_call(
        functools.partial(extend_add, n_dev, rows_blocks, cols_blocks),
        out_shape=(result, result),
        in_specs=[smem, smem, vmem, vmem],
        out_specs=(pl.BlockSpec(memory_space=pl.ANY), vmem),
        scratch_shapes=[pltpu.SemaphoreType.DMA((rows_blocks,))],
        compiler_params=params(),
        cost_estimate=pl.CostEstimate(flops=8 << 30, bytes_accessed=28 << 20, transcendentals=0),
        name="extend_add",
    )(order, starts, got, front)

    def product(p, a):
        return lax.dot_general(p, a, (((0,), (0,)), ((), ())), preferred_element_type=f32)

    real = product(panel.reshape(2 * height, samples), near.reshape(2 * height, width))
    imag = product(panel[0], near[1]) - product(panel[1], near[0])
    partial = jnp.stack([real.astype(bf16).reshape(n_row, -1, width), imag.astype(bf16).reshape(n_row, -1, width)], axis=1)
    arrived = lax.all_to_all(
        partial.reshape(n_row, 2 * samples // n_row, width), "row", split_axis=0, concat_axis=0, tiled=True
    )
    sample = arrived.astype(f32).sum(axis=0).reshape(2, samples // n_row, width)
    return assembled, sample


def solution(mesh):
    placed = (
        P(None, "row", "col"),
        P(BOTH, None, None, None),
        P(BOTH, None),
        P(BOTH),
        P(BOTH),
        P(None, "row", None),
    )
    return jax.shard_map(
        body,
        mesh=mesh,
        in_specs=placed,
        out_specs=(P(None, "row", "col"), P(None, "row", "col")),
        check_vma=False,
    )
```

time: 277 us -> 262 us (0.946)
  Pallas kernels: 23.5 us -> 8.66 us
    pallas_call x1, Pallas kernels: 13.8 us -> 2.95 us  [body(): pl.pallas_call(functools.partial(pack, n_dev), out_shape=jax.ShapeDtypeSt...]
    pallas_call x1, Pallas kernels: 9.68 us -> 5.71 us  [body(): pl.pallas_call(functools.partial(extend_add, n_dev, rows_blocks, cols_blo...]
where the time goes in v2:
time: 262 us; the launch traced here: 261 us
  blocking collectives  233 us (89%)
  matrix products  9.91 us (4%)
  Pallas kernels  8.66 us (3%)
  local copies, waits for them, and re-layouts  6.28 us (2%)
    all_to_all x1, blocking collectives, body(): got = lax.all_to_all(packed, BOTH, split_axis=0, concat_axis=0, tiled=True)  203 us
    all_to_all x1, blocking collectives, body(): lax.all_to_all(partial.reshape(n_row, 2 * samples // n_row, width), 'row'...  30 us
    dot_general x3, matrix products, product(): lax.dot_general(p, a, (((0,), (0,)), ((), ())), preferred_element_type=f32)  9.91 us
    pallas_call x1, Pallas kernels, body(): pl.pallas_call(functools.partial(extend_add, n_dev, rows_blocks, cols_blo...  5.71 us

profile of v2, /device:TPU:2, one launch (start us, length us, event | category | flops | bytes accessed | tf_op | source)
XLA Modules:
  0.0 260.7 jit_solution(3208445350485443669)
XLA Ops:
  1.3 0.0 copy-start
  1.3 3.4 %copy-done = bf16[128,2,128,128]{3,2,1,0:T(8,128)(2,1)S(1)} copy-done((bf16[128,2,128,128]{3,2,1,0:T(8,128)(2,1)S(1)}, bf16[128,2,128,128]{3,2,1,0:T(8,128)(2,1)}, u32[]{:S(2)}) %copy-start) | copy-done | bytes 8388632
  4.7 0.0 copy-start.1
  4.7 0.7 copy-done.1
  5.3 0.0 copy-start.2
  5.3 0.7 copy-done.2
  6.0 3.0 %pack.1 = bf16[128,520,128]{2,1,0:T(8,128)(2,1)S(1)} custom-call(s32[128]{0:T(128)S(1)} %bitcast.35, s32[128]{0:T(128)S(1)} %copy-done.2, s32[1]{0:T(128)S(6)} %copy.16.count, bf16[128,256,128]{2,1,0:T(8,128)(2,1)S(1)} %bitcast.34), custom_call_target="tpu_custom_call" | custom-call | flops 1048576 | bytes 16777216 | tf_op jit(solution)/shard_map/pack/pallas_call | solution.py:93
  8.9 0.0 slice-start.1
  8.9 203.0 %all_to_all.10.tiles = bf16[128,520,128]{2,1,0:T(8,128)(2,1)S(1)} all-to-all(bf16[128,520,128]{2,1,0:T(8,128)(2,1)S(1)} %pack.1), channel_id=1, replica_groups=mesh['row'=16,'col'=8] {'row','col'}, dimensions={0} | all-to-all | bytes 34078720 | tf_op jit(solution)/shard_map/all_to_all | solution.py:103
  211.9 1.6 slice_reduce_fusion.1
  213.5 0.1 convert_reduce_fusion.2.starts
  213.7 0.2 convert_reduce_fusion.1
  213.8 0.1 select_reduce_fusion.order
  214.0 0.0 slice-done
  214.0 0.0 slice-done.1
  214.0 5.7 %extend_add.1 = (bf16[2,2048,768]{2,1,0:T(8,128)(2,1)}, bf16[2,2048,768]{2,1,0:T(8,128)(2,1)S(1)}) custom-call(s32[256]{0:T(256)S(1)} %select_reduce_fusion.order, s32[97]{0:T(128)S(1)} %convert_reduce_fusion.2.starts, bf16[128,520,128]{2,1,0:T(8,128)(2,1)S(1)} %all_to_all.10.tiles, bf16[2,2048,768]{2,1,0:T(8,128)(2,1)S(1)} %bitcast.37), custom_call_target="tpu_custom_call" | custom-call | flops 8589934592 | bytes 29360128 | tf_op jit(solution)/shard_map/extend_add/pallas_call | solution.py:114
  219.7 0.0 copy-start.3
  219.7 6.0 %bitcast_convert_fusion = bf16[768,512]{0,1:T(8,128)(2,1)S(1)} fusion(bf16[2,2048,768]{2,1,0:T(8,128)(2,1)S(1)} %get-tuple-element.5, bf16[2,2048,512]{2,1,0:T(8,128)(2,1)} %param.11), kind=kOutput, calls=%fused_computation.12 | convolution fusion | flops 3221618688 | bytes 11272192 | tf_op jit(solution)/shard_map/dot_general | solution.py:126
  225.8 0.0 copy-done.3
  225.8 1.9 fusion
  227.7 1.9 subtract_convert_fusion
  229.7 0.2 pad_maximum_fusion
  229.8 30.0 %all_to_all.11 = bf16[16,64,768]{2,1,0:T(8,128)(2,1)S(1)} all-to-all(bf16[16,64,768]{2,1,0:T(8,128)(2,1)S(1)} %bitcast.38), channel_id=1, replica_groups=mesh['row'=16,'col'=8] {'row'}, dimensions={0} | all-to-all | bytes 3145728 | tf_op jit(solution)/shard_map/all_to_all | solution.py:131
  259.8 0.9 convert_reduce_fusion
  (3 shorter events, 0.0 us)
Async XLA Ops:
  1.3 3.4 %copy-start = (bf16[128,2,128,128]{3,2,1,0:T(8,128)(2,1)S(1)}, bf16[128,2,128,128]{3,2,1,0:T(8,128)(2,1)}, u32[]{:S(2)}) copy-start(bf16[128,2,128,128]{3,2,1,0:T(8,128)(2,1)} %param.7) | copy-start | bytes 25165828
  4.7 0.7 copy-start.1
  5.3 0.7 copy-start.2
  6.0 208.0 %slice-start = ((s8[6291456]{0:T(1024)(128)(4,1)}), s8[4194304]{0:T(1024)(128)(4,1)S(1)}, s32[]{:S(2)}) async-start(s8[6291456]{0:T(1024)(128)(4,1)} %bitcast.36), calls=%async_computation.2 | async-start | bytes 8388608
  8.9 205.1 %slice-start.1 = ((s8[6291456]{0:T(1024)(128)(4,1)}), s8[2097152]{0:T(1024)(128)(4,1)S(1)}, s32[]{:S(2)}) async-start(s8[6291456]{0:T(1024)(128)(4,1)} %bitcast.36), calls=%async_computation.3 | async-start | bytes 4194304
  219.7 6.1 %copy-start.3 = (bf16[2,2048,512]{2,1,0:T(8,128)(2,1)S(1)}, bf16[2,2048,512]{2,1,0:T(8,128)(2,1)}, u32[]{:S(2)}) copy-start(bf16[2,2048,512]{2,1,0:T(8,128)(2,1)} %param.11) | copy-start | bytes 12582916

commit v3 on v2

--- a/solution.py
+++ b/solution.py
@@ -11,7 +11,7 @@
 VMEM_LIMIT = 4 * 1024 * 1024
 
 
-def pack(n_dev, owner, spot, count, tiles, out, seen, spots):
+def pack(n_dev, n_spots, target, count, tiles, out, seen, spots):
     def clear(d, carry):
         seen[d] = 0
         for k in range(2):
@@ -21,10 +21,10 @@
     lax.fori_loop(0, n_dev, clear, 0, unroll=8)
 
     def route(j, carry):
-        to = owner[j]
+        to = target[j] // n_spots
         rank = seen[to]
         seen[to] = rank + 1
-        spots[to * 2 + rank] = spot[j]
+        spots[to * 2 + rank] = target[j] - to * n_spots
         out[to, pl.ds(pl.multiple_of(rank * 256, 256), 256), :] = tiles[j]
         return carry
 
@@ -51,17 +51,17 @@
             first, last = starts[step * cols_blocks + c], starts[step * cols_blocks + c + 1]
             columns = slice(c * 128, (c + 1) * 128)
 
-            def add(p, values):
-                slot = order[p]
+            def add(p, carry):
+                slot, values = carry
                 rank = slot // n_dev
                 source = slot - rank * n_dev
-                return tuple(
+                return order[p + 1], tuple(
                     value + tiles[source, pl.ds(pl.multiple_of(rank * 256 + part * 128, 128), 128), :].astype(jnp.float32)
                     for part, value in enumerate(values)
                 )
 
             values = tuple(front[part, rows(step), columns].astype(jnp.float32) for part in range(2))
-            for part, value in enumerate(lax.fori_loop(first, last, add, values)):
+            for part, value in enumerate(lax.fori_loop(first, last, add, (order[first], values))[1]):
                 near[part, rows(step), columns] = value.astype(jnp.bfloat16)
         put(step).start()
         return carry
@@ -89,17 +89,18 @@
     params = functools.partial(pltpu.CompilerParams, vmem_limit_bytes=VMEM_LIMIT)
     n_slots = 2 * n_dev
     message = 4 * tile + 8
+    spot_range = pl.next_power_of_2(n_spots)
 
     packed = pl.pallas_call(
-        functools.partial(pack, n_dev),
+        functools.partial(pack, n_dev, spot_range),
         out_shape=jax.ShapeDtypeStruct((n_dev, message, tile), bf16),
-        in_specs=[smem, smem, smem, vmem],
+        in_specs=[smem, smem, vmem],
         out_specs=vmem,
         scratch_shapes=[pltpu.SMEM((n_dev,), i32), pltpu.SMEM((n_slots,), i32)],
         compiler_params=params(),
         cost_estimate=pl.CostEstimate(flops=1 << 20, bytes_accessed=2 * n_dev * 65536, transcendentals=0),
         name="pack",
-    )(tile_owner[:, 0], tile_spot, tile_count, child_tiles.reshape(n_tiles, 2 * tile, tile))
+    )(tile_owner[:, 0] * spot_range + tile_spot, tile_count, child_tiles.reshape(n_tiles, 2 * tile, tile))
     got = lax.all_to_all(packed, BOTH, split_axis=0, concat_axis=0, tiled=True)
 
     spots = jnp.concatenate([got[:, 4 * tile, 0], got[:, 4 * tile, 1]]).astype(i32)
@@ -107,7 +108,7 @@
     spots = jnp.where(spots >= 0, spots, n_spots)
     key = spots * n_slots + slot
     place = jnp.sum((key[None, :] < key[:, None]).astype(i32), axis=1)
-    order = jnp.sum(jnp.where(place[None, :] == slot[:, None], slot[None, :], 0), axis=1)
+    order = jnp.sum(jnp.where(place[None, :] == jnp.arange(n_slots + 1)[:, None], slot[None, :], 0), axis=1)
     starts = jnp.sum((spots[None, :] < jnp.arange(n_spots + 1)[:, None]).astype(i32), axis=1)
 
     result = jax.ShapeDtypeStruct((2, height, width), bf16)
@@ -125,7 +126,7 @@
     def product(p, a):
         return lax.dot_general(p, a, (((0,), (0,)), ((), ())), preferred_element_type=f32)
 
-    real = product(panel.reshape(2 * height, samples), near.reshape(2 * height, width))
+    real = product(panel[0], near[0]) + product(panel[1], near[1])
     imag = product(panel[0], near[1]) - product(panel[1], near[0])
     partial = jnp.stack([real.astype(bf16).reshape(n_row, -1, width), imag.astype(bf16).reshape(n_row, -1, width)], axis=1)
     arrived = lax.all_to_all(

time: 262 us -> 260 us (level)
    dot_general x3 -> x4, matrix products: 9.91 us -> 7.46 us  [product(): lax.dot_general(p, a, (((0,), (0,)), ((), ())), preferred_element_type=f32)]
where the time goes in v3:
time: 260 us; the launch traced here: 258 us
  blocking collectives  233 us (90%)
  Pallas kernels  8.93 us (3%)
  matrix products  7.46 us (3%)
  local copies, waits for them, and re-layouts  4.98 us (2%)
    all_to_all x1, blocking collectives, body(): got = lax.all_to_all(packed, BOTH, split_axis=0, concat_axis=0, tiled=True)  203 us
    all_to_all x1, blocking collectives, body(): lax.all_to_all(partial.reshape(n_row, 2 * samples // n_row, width), 'row'...  30.2 us
    dot_general x4, matrix products, product(): lax.dot_general(p, a, (((0,), (0,)), ((), ())), preferred_element_type=f32)  7.46 us
    pallas_call x1, Pallas kernels, body(): pl.pallas_call(functools.partial(extend_add, n_dev, rows_blocks, cols_blo...  5.32 us

profile of v3, /device:TPU:2, one launch (start us, length us, event | category | flops | bytes accessed | tf_op | source)
XLA Modules:
  0.0 258.1 jit_solution(6602425385420231278)
XLA Ops:
  1.3 0.7 bitcast_add_fusion.target
  2.0 0.0 copy-start
  2.0 3.4 %copy-done = bf16[128,2,128,128]{3,2,1,0:T(8,128)(2,1)S(1)} copy-done((bf16[128,2,128,128]{3,2,1,0:T(8,128)(2,1)S(1)}, bf16[128,2,128,128]{3,2,1,0:T(8,128)(2,1)}, u32[]{:S(2)}) %copy-start) | copy-done | bytes 8388632
  5.3 0.0 slice-start
  5.3 3.6 %pack.1 = bf16[128,520,128]{2,1,0:T(8,128)(2,1)S(1)} custom-call(s32[128]{0:T(128)S(1)} %bitcast_add_fusion.target, s32[1]{0:T(128)S(6)} %copy.12.count, bf16[128,256,128]{2,1,0:T(8,128)(2,1)S(1)} %bitcast.43), custom_call_target="tpu_custom_call" | custom-call | flops 1048576 | bytes 16777216 | tf_op jit(solution)/shard_map/pack/pallas_call | solution.py:94
  9.0 0.0 slice-start.1
  9.0 203.0 %all_to_all.10.tiles = bf16[128,520,128]{2,1,0:T(8,128)(2,1)S(1)} all-to-all(bf16[128,520,128]{2,1,0:T(8,128)(2,1)S(1)} %pack.1), channel_id=1, replica_groups=mesh['row'=16,'col'=8] {'row','col'}, dimensions={0} | all-to-all | bytes 34078720 | tf_op jit(solution)/shard_map/all_to_all | solution.py:104
  211.9 1.6 slice_reduce_fusion.1
  213.5 0.1 convert_reduce_fusion.2.starts
  213.7 0.2 convert_reduce_fusion.1
  213.8 0.2 select_reduce_fusion.order
  214.0 0.0 slice-done
  214.0 0.0 slice-done.1
  214.0 0.0 copy-start.1
  214.0 5.3 %extend_add.1 = (bf16[2,2048,768]{2,1,0:T(8,128)(2,1)}, bf16[2,2048,768]{2,1,0:T(8,128)(2,1)S(1)}) custom-call(s32[257]{0:T(512)S(1)} %select_reduce_fusion.order, s32[97]{0:T(128)S(1)} %convert_reduce_fusion.2.starts, bf16[128,520,128]{2,1,0:T(8,128)(2,1)S(1)} %all_to_all.10.tiles, bf16[2,2048,768]{2,1,0:T(8,128)(2,1)S(1)} %bitcast.45), custom_call_target="tpu_custom_call" | custom-call | flops 8589934592 | bytes 29360128 | tf_op jit(solution)/shard_map/extend_add/pallas_call | solution.py:115
  219.4 0.0 copy-done.1
  219.4 1.9 fusion
  221.2 1.9 fusion.2
  223.1 1.9 subtract_convert_fusion
  225.0 1.9 add_convert_fusion
  226.9 0.2 pad_maximum_fusion
  227.0 30.2 %all_to_all.11 = bf16[16,64,768]{2,1,0:T(8,128)(2,1)S(1)} all-to-all(bf16[16,64,768]{2,1,0:T(8,128)(2,1)S(1)} %bitcast.46), channel_id=1, replica_groups=mesh['row'=16,'col'=8] {'row'}, dimensions={0} | all-to-all | bytes 3145728 | tf_op jit(solution)/shard_map/all_to_all | solution.py:132
  257.2 0.9 convert_reduce_fusion
  (2 shorter events, 0.0 us)
Async XLA Ops:
  2.0 3.4 %copy-start = (bf16[128,2,128,128]{3,2,1,0:T(8,128)(2,1)S(1)}, bf16[128,2,128,128]{3,2,1,0:T(8,128)(2,1)}, u32[]{:S(2)}) copy-start(bf16[128,2,128,128]{3,2,1,0:T(8,128)(2,1)} %param.7) | copy-start | bytes 25165828
  5.3 208.7 %slice-start = ((s8[6291456]{0:T(1024)(128)(4,1)}), s8[4194304]{0:T(1024)(128)(4,1)S(1)}, s32[]{:S(2)}) async-start(s8[6291456]{0:T(1024)(128)(4,1)} %bitcast.44), calls=%async_computation.2 | async-start | bytes 8388608
  9.0 205.0 %slice-start.1 = ((s8[6291456]{0:T(1024)(128)(4,1)}), s8[2097152]{0:T(1024)(128)(4,1)S(1)}, s32[]{:S(2)}) async-start(s8[6291456]{0:T(1024)(128)(4,1)} %bitcast.44), calls=%async_computation.3 | async-start | bytes 4194304
  214.0 5.3 %copy-start.1 = (bf16[2,2048,512]{2,1,0:T(8,128)(2,1)S(1)}, bf16[2,2048,512]{2,1,0:T(8,128)(2,1)}, u32[]{:S(2)}) copy-start(bf16[2,2048,512]{2,1,0:T(8,128)(2,1)} %param.11) | copy-start | bytes 12582916

commit v4 on v3

--- a/solution.py
+++ b/solution.py
@@ -28,7 +28,9 @@
         out[to, pl.ds(pl.multiple_of(rank * 256, 256), 256), :] = tiles[j]
         return carry
 
-    lax.fori_loop(0, jnp.minimum(count[0], tiles.shape[0]), route, 0)
+    live = jnp.minimum(count[0], tiles.shape[0])
+    lax.fori_loop(0, live // 4, lambda i, carry: functools.reduce(lambda c, u: route(i * 4 + u, c), range(4), carry), 0)
+    lax.fori_loop(live // 4 * 4, live, route, 0)
     lane = lax.broadcasted_iota(jnp.int32, (8, 128), 1)
 
     def label(d, carry):
@@ -51,18 +53,29 @@
             first, last = starts[step * cols_blocks + c], starts[step * cols_blocks + c + 1]
             columns = slice(c * 128, (c + 1) * 128)
 
-            def add(p, carry):
-                slot, values = carry
+            def read(slot, part):
                 rank = slot // n_dev
-                source = slot - rank * n_dev
-                return order[p + 1], tuple(
-                    value + tiles[source, pl.ds(pl.multiple_of(rank * 256 + part * 128, 128), 128), :].astype(jnp.float32)
-                    for part, value in enumerate(values)
-                )
+                here = pl.ds(pl.multiple_of(rank * 256 + part * 128, 128), 128)
+                return tiles[slot - rank * n_dev, here, :].astype(jnp.float32)
 
-            values = tuple(front[part, rows(step), columns].astype(jnp.float32) for part in range(2))
-            for part, value in enumerate(lax.fori_loop(first, last, add, (order[first], values))[1]):
+            def add(p, values):
+                slot = order[p]
+                return tuple(value + read(slot, part) for part, value in enumerate(values))
+
+            values = [front[part, rows(step), columns].astype(jnp.float32) for part in range(2)]
+            for k in range(2):
+                slot = order[first + k]
+                here = jnp.full((128, 128), last - first, jnp.int32) > k
+                values = [value + jnp.where(here, read(slot, part), 0.0) for part, value in enumerate(values)]
+            for part, value in enumerate(values):
                 near[part, rows(step), columns] = value.astype(jnp.bfloat16)
+
+            @pl.when(last - first > 2)
+            def _():
+                more = lax.fori_loop(first + 2, last, add, tuple(values))
+                for part, value in enumerate(more):
+                    near[part, rows(step), columns] = value.astype(jnp.bfloat16)
+
         put(step).start()
         return carry
 
@@ -108,7 +121,7 @@
     spots = jnp.where(spots >= 0, spots, n_spots)
     key = spots * n_slots + slot
     place = jnp.sum((key[None, :] < key[:, None]).astype(i32), axis=1)
-    order = jnp.sum(jnp.where(place[None, :] == jnp.arange(n_slots + 1)[:, None], slot[None, :], 0), axis=1)
+    order = jnp.sum(jnp.where(place[None, :] == jnp.arange(n_slots + 2)[:, None], slot[None, :], 0), axis=1)
     starts = jnp.sum((spots[None, :] < jnp.arange(n_spots + 1)[:, None]).astype(i32), axis=1)
 
     result = jax.ShapeDtypeStruct((2, height, width), bf16)

time: 260 us -> 259 us (level)
  no operation moved by 1% of the time
where the time goes in v4:
time: 259 us
  blocking collectives  234 us (90%)
  Pallas kernels  9.48 us (4%)
  matrix products  7.46 us (3%)
  local copies, waits for them, and re-layouts  4.98 us (2%)
    all_to_all x1, blocking collectives, body(): got = lax.all_to_all(packed, BOTH, split_axis=0, concat_axis=0, tiled=True)  203 us
    all_to_all x1, blocking collectives, body(): lax.all_to_all(partial.reshape(n_row, 2 * samples // n_row, width), 'row'...  30.6 us
    dot_general x4, matrix products, product(): lax.dot_general(p, a, (((0,), (0,)), ((), ())), preferred_element_type=f32)  7.46 us
    pallas_call x1, Pallas kernels, body(): pl.pallas_call(functools.partial(extend_add, n_dev, rows_blocks, cols_blo...  6.71 us

profile of v4, /device:TPU:2, one launch (start us, length us, event | category | flops | bytes accessed | tf_op | source)
XLA Modules:
  0.0 259.3 jit_solution(5904496820472149876)
XLA Ops:
  1.3 0.7 bitcast_add_fusion.target
  2.0 0.0 copy-start
  2.0 3.4 %copy-done = bf16[128,2,128,128]{3,2,1,0:T(8,128)(2,1)S(1)} copy-done((bf16[128,2,128,128]{3,2,1,0:T(8,128)(2,1)S(1)}, bf16[128,2,128,128]{3,2,1,0:T(8,128)(2,1)}, u32[]{:S(2)}) %copy-start) | copy-done | bytes 8388632
  5.3 0.0 slice-start
  5.3 2.8 %pack.1 = bf16[128,520,128]{2,1,0:T(8,128)(2,1)S(1)} custom-call(s32[128]{0:T(128)S(1)} %bitcast_add_fusion.target, s32[1]{0:T(128)S(6)} %copy.12.count, bf16[128,256,128]{2,1,0:T(8,128)(2,1)S(1)} %bitcast.43), custom_call_target="tpu_custom_call" | custom-call | flops 1048576 | bytes 16777216 | tf_op jit(solution)/shard_map/pack/pallas_call | solution.py:107
  8.1 0.0 slice-start.1
  8.1 203.2 %all_to_all.10.tiles = bf16[128,520,128]{2,1,0:T(8,128)(2,1)S(1)} all-to-all(bf16[128,520,128]{2,1,0:T(8,128)(2,1)S(1)} %pack.1), channel_id=1, replica_groups=mesh['row'=16,'col'=8] {'row','col'}, dimensions={0} | all-to-all | bytes 34078720 | tf_op jit(solution)/shard_map/all_to_all | solution.py:117
  211.3 1.6 slice_reduce_fusion.1
  212.9 0.1 convert_reduce_fusion.2.starts
  213.0 0.2 convert_reduce_fusion.1
  213.2 0.2 select_reduce_fusion.order
  213.3 0.0 slice-done
  213.4 0.0 slice-done.1
  213.4 0.0 copy-start.1
  213.4 6.7 %extend_add.1 = (bf16[2,2048,768]{2,1,0:T(8,128)(2,1)}, bf16[2,2048,768]{2,1,0:T(8,128)(2,1)S(1)}) custom-call(s32[258]{0:T(512)S(1)} %select_reduce_fusion.order, s32[97]{0:T(128)S(1)} %convert_reduce_fusion.2.starts, bf16[128,520,128]{2,1,0:T(8,128)(2,1)S(1)} %all_to_all.10.tiles, bf16[2,2048,768]{2,1,0:T(8,128)(2,1)S(1)} %bitcast.45), custom_call_target="tpu_custom_call" | custom-call | flops 8589934592 | bytes 29360128 | tf_op jit(solution)/shard_map/extend_add/pallas_call | solution.py:128
  220.1 0.0 copy-done.1
  220.1 1.9 fusion
  222.0 1.9 fusion.2
  223.9 1.9 subtract_convert_fusion
  225.7 1.9 add_convert_fusion
  227.6 0.2 pad_maximum_fusion
  227.8 30.6 %all_to_all.11 = bf16[16,64,768]{2,1,0:T(8,128)(2,1)S(1)} all-to-all(bf16[16,64,768]{2,1,0:T(8,128)(2,1)S(1)} %bitcast.46), channel_id=1, replica_groups=mesh['row'=16,'col'=8] {'row'}, dimensions={0} | all-to-all | bytes 3145728 | tf_op jit(solution)/shard_map/all_to_all | solution.py:145
  258.4 0.9 convert_reduce_fusion
  (2 shorter events, 0.0 us)
Async XLA Ops:
  2.0 3.4 %copy-start = (bf16[128,2,128,128]{3,2,1,0:T(8,128)(2,1)S(1)}, bf16[128,2,128,128]{3,2,1,0:T(8,128)(2,1)}, u32[]{:S(2)}) copy-start(bf16[128,2,128,128]{3,2,1,0:T(8,128)(2,1)} %param.7) | copy-start | bytes 25165828
  5.3 208.0 %slice-start = ((s8[6291456]{0:T(1024)(128)(4,1)}), s8[4194304]{0:T(1024)(128)(4,1)S(1)}, s32[]{:S(2)}) async-start(s8[6291456]{0:T(1024)(128)(4,1)} %bitcast.44), calls=%async_computation.2 | async-start | bytes 8388608
  8.1 205.2 %slice-start.1 = ((s8[6291456]{0:T(1024)(128)(4,1)}), s8[2097152]{0:T(1024)(128)(4,1)S(1)}, s32[]{:S(2)}) async-start(s8[6291456]{0:T(1024)(128)(4,1)} %bitcast.44), calls=%async_computation.3 | async-start | bytes 4194304
  213.4 6.7 %copy-start.1 = (bf16[2,2048,512]{2,1,0:T(8,128)(2,1)S(1)}, bf16[2,2048,512]{2,1,0:T(8,128)(2,1)}, u32[]{:S(2)}) copy-start(bf16[2,2048,512]{2,1,0:T(8,128)(2,1)} %param.11) | copy-start | bytes 12582916

commit v5 on v4

--- a/solution.py
+++ b/solution.py
@@ -62,19 +62,17 @@
                 slot = order[p]
                 return tuple(value + read(slot, part) for part, value in enumerate(values))
 
-            values = [front[part, rows(step), columns].astype(jnp.float32) for part in range(2)]
-            for k in range(2):
-                slot = order[first + k]
-                here = jnp.full((128, 128), last - first, jnp.int32) > k
-                values = [value + jnp.where(here, read(slot, part), 0.0) for part, value in enumerate(values)]
+            def add_two(i, values):
+                p = first + i * 2
+                slots = order[p], order[p + 1]
+                return tuple(value + read(slots[0], part) + read(slots[1], part) for part, value in enumerate(values))
+
+            values = tuple(front[part, rows(step), columns].astype(jnp.float32) for part in range(2))
+            pairs = (last - first) // 2
+            values = lax.fori_loop(0, pairs, add_two, values)
+            values = lax.fori_loop(first + pairs * 2, last, add, values)
             for part, value in enumerate(values):
                 near[part, rows(step), columns] = value.astype(jnp.bfloat16)
-
-            @pl.when(last - first > 2)
-            def _():
-                more = lax.fori_loop(first + 2, last, add, tuple(values))
-                for part, value in enumerate(more):
-                    near[part, rows(step), columns] = value.astype(jnp.bfloat16)
 
         put(step).start()
         return carry
@@ -121,7 +119,7 @@
     spots = jnp.where(spots >= 0, spots, n_spots)
     key = spots * n_slots + slot
     place = jnp.sum((key[None, :] < key[:, None]).astype(i32), axis=1)
-    order = jnp.sum(jnp.where(place[None, :] == jnp.arange(n_slots + 2)[:, None], slot[None, :], 0), axis=1)
+    order = jnp.sum(jnp.where(place[None, :] == slot[:, None], slot[None, :], 0), axis=1)
     starts = jnp.sum((spots[None, :] < jnp.arange(n_spots + 1)[:, None]).astype(i32), axis=1)
 
     result = jax.ShapeDtypeStruct((2, height, width), bf16)

time: 259 us -> 257 us (level)
  no operation moved by 1% of the time
where the time goes in v5:
time: 257 us
  blocking collectives  232 us (90%)
  Pallas kernels  9.01 us (4%)
  matrix products  7.45 us (3%)
  local copies, waits for them, and re-layouts  4.98 us (2%)
    all_to_all x1, blocking collectives, body(): got = lax.all_to_all(packed, BOTH, split_axis=0, concat_axis=0, tiled=True)  203 us
    all_to_all x1, blocking collectives, body(): lax.all_to_all(partial.reshape(n_row, 2 * samples // n_row, width), 'row'...  29.2 us
    dot_general x4, matrix products, product(): lax.dot_general(p, a, (((0,), (0,)), ((), ())), preferred_element_type=f32)  7.45 us
    pallas_call x1, Pallas kernels, body(): pl.pallas_call(functools.partial(extend_add, n_dev, rows_blocks, cols_blo...  6.33 us

profile of v5, /device:TPU:2, one launch (start us, length us, event | category | flops | bytes accessed | tf_op | source)
XLA Modules:
  0.0 257.2 jit_solution(12769295147038904190)
XLA Ops:
  1.3 0.7 bitcast_add_fusion.target
  2.0 0.0 copy-start
  2.0 3.4 %copy-done = bf16[128,2,128,128]{3,2,1,0:T(8,128)(2,1)S(1)} copy-done((bf16[128,2,128,128]{3,2,1,0:T(8,128)(2,1)S(1)}, bf16[128,2,128,128]{3,2,1,0:T(8,128)(2,1)}, u32[]{:S(2)}) %copy-start) | copy-done | bytes 8388632
  5.3 0.0 slice-start
  5.3 2.7 %pack.1 = bf16[128,520,128]{2,1,0:T(8,128)(2,1)S(1)} custom-call(s32[128]{0:T(128)S(1)} %bitcast_add_fusion.target, s32[1]{0:T(128)S(6)} %copy.12.count, bf16[128,256,128]{2,1,0:T(8,128)(2,1)S(1)} %bitcast.43), custom_call_target="tpu_custom_call" | custom-call | flops 1048576 | bytes 16777216 | tf_op jit(solution)/shard_map/pack/pallas_call | solution.py:105
  8.0 0.0 slice-start.1
  8.0 203.0 %all_to_all.10.tiles = bf16[128,520,128]{2,1,0:T(8,128)(2,1)S(1)} all-to-all(bf16[128,520,128]{2,1,0:T(8,128)(2,1)S(1)} %pack.1), channel_id=1, replica_groups=mesh['row'=16,'col'=8] {'row','col'}, dimensions={0} | all-to-all | bytes 34078720 | tf_op jit(solution)/shard_map/all_to_all | solution.py:115
  211.1 1.6 slice_reduce_fusion.1
  212.7 0.1 convert_reduce_fusion.2.starts
  212.8 0.2 convert_reduce_fusion.1
  213.0 0.1 select_reduce_fusion.order
  213.1 0.0 slice-done
  213.1 0.0 slice-done.1
  213.1 0.0 copy-start.1
  213.1 6.3 %extend_add.1 = (bf16[2,2048,768]{2,1,0:T(8,128)(2,1)}, bf16[2,2048,768]{2,1,0:T(8,128)(2,1)S(1)}) custom-call(s32[256]{0:T(256)S(1)} %select_reduce_fusion.order, s32[97]{0:T(128)S(1)} %convert_reduce_fusion.2.starts, bf16[128,520,128]{2,1,0:T(8,128)(2,1)S(1)} %all_to_all.10.tiles, bf16[2,2048,768]{2,1,0:T(8,128)(2,1)S(1)} %bitcast.45), custom_call_target="tpu_custom_call" | custom-call | flops 8589934592 | bytes 29360128 | tf_op jit(solution)/shard_map/extend_add/pallas_call | solution.py:126
  219.5 0.0 copy-done.1
  219.5 1.9 fusion
  221.4 1.9 fusion.2
  223.2 1.9 subtract_convert_fusion
  225.1 1.9 add_convert_fusion
  227.0 0.2 pad_maximum_fusion
  227.1 29.2 %all_to_all.11 = bf16[16,64,768]{2,1,0:T(8,128)(2,1)S(1)} all-to-all(bf16[16,64,768]{2,1,0:T(8,128)(2,1)S(1)} %bitcast.46), channel_id=1, replica_groups=mesh['row'=16,'col'=8] {'row'}, dimensions={0} | all-to-all | bytes 3145728 | tf_op jit(solution)/shard_map/all_to_all | solution.py:143
  256.3 0.9 convert_reduce_fusion
  (2 shorter events, 0.0 us)
Async XLA Ops:
  2.0 3.4 %copy-start = (bf16[128,2,128,128]{3,2,1,0:T(8,128)(2,1)S(1)}, bf16[128,2,128,128]{3,2,1,0:T(8,128)(2,1)}, u32[]{:S(2)}) copy-start(bf16[128,2,128,128]{3,2,1,0:T(8,128)(2,1)} %param.7) | copy-start | bytes 25165828
  5.3 207.8 %slice-start = ((s8[6291456]{0:T(1024)(128)(4,1)}), s8[4194304]{0:T(1024)(128)(4,1)S(1)}, s32[]{:S(2)}) async-start(s8[6291456]{0:T(1024)(128)(4,1)} %bitcast.44), calls=%async_computation.2 | async-start | bytes 8388608
  8.0 205.1 %slice-start.1 = ((s8[6291456]{0:T(1024)(128)(4,1)}), s8[2097152]{0:T(1024)(128)(4,1)S(1)}, s32[]{:S(2)}) async-start(s8[6291456]{0:T(1024)(128)(4,1)} %bitcast.44), calls=%async_computation.3 | async-start | bytes 4194304
  213.1 6.4 %copy-start.1 = (bf16[2,2048,512]{2,1,0:T(8,128)(2,1)S(1)}, bf16[2,2048,512]{2,1,0:T(8,128)(2,1)}, u32[]{:S(2)}) copy-start(bf16[2,2048,512]{2,1,0:T(8,128)(2,1)} %param.11) | copy-start | bytes 12582916

commit v6 on v3

--- a/solution.py
+++ b/solution.py
@@ -28,7 +28,9 @@
         out[to, pl.ds(pl.multiple_of(rank * 256, 256), 256), :] = tiles[j]
         return carry
 
-    lax.fori_loop(0, jnp.minimum(count[0], tiles.shape[0]), route, 0)
+    live = jnp.minimum(count[0], tiles.shape[0])
+    lax.fori_loop(0, live // 4, lambda i, carry: functools.reduce(lambda c, u: route(i * 4 + u, c), range(4), carry), 0)
+    lax.fori_loop(live // 4 * 4, live, route, 0)
     lane = lax.broadcasted_iota(jnp.int32, (8, 128), 1)
 
     def label(d, carry):

time: 260 us -> 258 us (level)
  no operation moved by 1% of the time
where the time goes in v6:
time: 258 us; the launch traced here: 257 us
  blocking collectives  233 us (90%)
  Pallas kernels  8.31 us (3%)
  matrix products  7.46 us (3%)
  local copies, waits for them, and re-layouts  4.98 us (2%)
    all_to_all x1, blocking collectives, body(): got = lax.all_to_all(packed, BOTH, split_axis=0, concat_axis=0, tiled=True)  203 us
    all_to_all x1, blocking collectives, body(): lax.all_to_all(partial.reshape(n_row, 2 * samples // n_row, width), 'row'...  29.7 us
    dot_general x4, matrix products, product(): lax.dot_general(p, a, (((0,), (0,)), ((), ())), preferred_element_type=f32)  7.46 us
    pallas_call x1, Pallas kernels, body(): pl.pallas_call(functools.partial(extend_add, n_dev, rows_blocks, cols_blo...  5.89 us

profile of v6, /device:TPU:2, one launch (start us, length us, event | category | flops | bytes accessed | tf_op | source)
XLA Modules:
  0.0 257.4 jit_solution(12060408740104051483)
XLA Ops:
  1.3 0.7 bitcast_add_fusion.target
  2.0 0.0 copy-start
  2.0 3.4 %copy-done = bf16[128,2,128,128]{3,2,1,0:T(8,128)(2,1)S(1)} copy-done((bf16[128,2,128,128]{3,2,1,0:T(8,128)(2,1)S(1)}, bf16[128,2,128,128]{3,2,1,0:T(8,128)(2,1)}, u32[]{:S(2)}) %copy-start) | copy-done | bytes 8388632
  5.3 0.0 slice-start
  5.3 2.4 pack.1
  7.8 0.0 slice-start.1
  7.8 203.4 %all_to_all.10.tiles = bf16[128,520,128]{2,1,0:T(8,128)(2,1)S(1)} all-to-all(bf16[128,520,128]{2,1,0:T(8,128)(2,1)S(1)} %pack.1), channel_id=1, replica_groups=mesh['row'=16,'col'=8] {'row','col'}, dimensions={0} | all-to-all | bytes 34078720 | tf_op jit(solution)/shard_map/all_to_all | solution.py:106
  211.1 1.6 slice_reduce_fusion.1
  212.7 0.1 convert_reduce_fusion.2.starts
  212.9 0.2 convert_reduce_fusion.1
  213.0 0.2 select_reduce_fusion.order
  213.2 0.0 slice-done
  213.2 0.0 slice-done.1
  213.2 0.0 copy-start.1
  213.2 5.9 %extend_add.1 = (bf16[2,2048,768]{2,1,0:T(8,128)(2,1)}, bf16[2,2048,768]{2,1,0:T(8,128)(2,1)S(1)}) custom-call(s32[257]{0:T(512)S(1)} %select_reduce_fusion.order, s32[97]{0:T(128)S(1)} %convert_reduce_fusion.2.starts, bf16[128,520,128]{2,1,0:T(8,128)(2,1)S(1)} %all_to_all.10.tiles, bf16[2,2048,768]{2,1,0:T(8,128)(2,1)S(1)} %bitcast.45), custom_call_target="tpu_custom_call" | custom-call | flops 8589934592 | bytes 29360128 | tf_op jit(solution)/shard_map/extend_add/pallas_call | solution.py:117
  219.1 0.0 copy-done.1
  219.1 1.9 fusion
  221.0 1.9 fusion.2
  222.9 1.9 subtract_convert_fusion
  224.8 1.9 add_convert_fusion
  226.6 0.2 pad_maximum_fusion
  226.8 29.7 %all_to_all.11 = bf16[16,64,768]{2,1,0:T(8,128)(2,1)S(1)} all-to-all(bf16[16,64,768]{2,1,0:T(8,128)(2,1)S(1)} %bitcast.46), channel_id=1, replica_groups=mesh['row'=16,'col'=8] {'row'}, dimensions={0} | all-to-all | bytes 3145728 | tf_op jit(solution)/shard_map/all_to_all | solution.py:134
  256.5 0.9 convert_reduce_fusion
  (2 shorter events, 0.0 us)
Async XLA Ops:
  2.0 3.4 %copy-start = (bf16[128,2,128,128]{3,2,1,0:T(8,128)(2,1)S(1)}, bf16[128,2,128,128]{3,2,1,0:T(8,128)(2,1)}, u32[]{:S(2)}) copy-start(bf16[128,2,128,128]{3,2,1,0:T(8,128)(2,1)} %param.7) | copy-start | bytes 25165828
  5.3 207.9 %slice-start = ((s8[6291456]{0:T(1024)(128)(4,1)}), s8[4194304]{0:T(1024)(128)(4,1)S(1)}, s32[]{:S(2)}) async-start(s8[6291456]{0:T(1024)(128)(4,1)} %bitcast.44), calls=%async_computation.2 | async-start | bytes 8388608
  7.8 205.4 %slice-start.1 = ((s8[6291456]{0:T(1024)(128)(4,1)}), s8[2097152]{0:T(1024)(128)(4,1)S(1)}, s32[]{:S(2)}) async-start(s8[6291456]{0:T(1024)(128)(4,1)} %bitcast.44), calls=%async_computation.3 | async-start | bytes 4194304
  213.2 5.9 %copy-start.1 = (bf16[2,2048,512]{2,1,0:T(8,128)(2,1)S(1)}, bf16[2,2048,512]{2,1,0:T(8,128)(2,1)}, u32[]{:S(2)}) copy-start(bf16[2,2048,512]{2,1,0:T(8,128)(2,1)} %param.11) | copy-start | bytes 12582916
